TPU v7x, 32 devices: a whole 2x2x4 slice. The times are simulated.
32 devices in a mesh: seq: 8 (over y, x, core), fsdp: 4 (over z).
Axes of the slice: x: 2, y: 2, z: 4, core: 2. Of those that a mesh axis runs over, the one named last changes fastest.
Arguments:
- hidden: bfloat16 [4096, 8192], P(('seq', 'fsdp')), may hold values from -6 to 6
- kv_blocks: bfloat16 [8192, 1024], P('fsdp'), may hold values from -0.0625 to 0.0625
- kv_scale: float32 [64, 8], P('fsdp'), may hold values from 0.5 to 2
- queries: bfloat16 [4096, 4096], P(('seq', 'fsdp')), may hold values from -24 to 24
- grad_out: bfloat16 [4096, 4096], P(('seq', 'fsdp')), may hold values from -6 to 6
Outputs:
- attn_out: bfloat16 [4096, 4096], P(('seq', 'fsdp'))
- grad_queries: bfloat16 [4096, 4096], P(('seq', 'fsdp'))
- grad_hidden: bfloat16 [4096, 8192], P(('seq', 'fsdp'))
- weight_grad: float32 [8192, 1024], P('fsdp')
All inputs are finite; a program needn't handle non-finite values.
Results may differ from a plain program's by a relative error of at most 0.0075.
The roundings to bfloat16 on the way count: a program that leaves them out, or rounds other values in their place, can miss the bound.
Values may be sent and summed in bfloat16 or wider, within the bound.
A program may use at most 128 MiB of HBM per device.

v0:
```python
import jax
import jax.numpy as jnp
from jax import lax
from jax.sharding import PartitionSpec as P

HEADS = 32
KV_HEADS = 4
HEAD = 128
QB = 128
NEG = -1e30


def shifted(block, axis, distance):
    devices = range(lax.axis_size(axis))
    route = [(i - distance, i) for i in devices if i - distance in devices]
    return lax.ppermute(block, axis, route)


def dequantize(blocks, scale):
    rows, cols = blocks.shape
    grid = blocks.astype(jnp.float32).reshape(scale.shape[0], QB, scale.shape[1], QB)
    return (grid * scale[:, None, :, None]).reshape(rows, cols).astype(jnp.bfloat16)


def attend_group(operands, allowed):
    qgrp, kgrp, vgrp, ggrp = operands
    factor = 1.0 / float(HEAD) ** 0.5
    scores = jnp.einsum("rhd,kd->rhk", qgrp, kgrp, preferred_element_type=jnp.float32) * factor
    scores = jnp.where(allowed[:, None, :], scores, NEG)
    top = jnp.max(scores, axis=-1, keepdims=True)
    expd = jnp.exp(scores - top)
    probs = expd / jnp.sum(expd, axis=-1, keepdims=True)
    probs_b = probs.astype(jnp.bfloat16)
    output = jnp.einsum("rhk,kd->rhd", probs_b, vgrp, preferred_element_type=jnp.float32).astype(
        jnp.bfloat16
    )
    dprobs = jnp.einsum("rhd,kd->rhk", ggrp, vgrp, preferred_element_type=jnp.float32)
    delta = jnp.sum(probs * dprobs, axis=-1, keepdims=True)
    dscores = (probs * (dprobs - delta) * factor).astype(jnp.bfloat16)
    gradq = jnp.einsum("rhk,kd->rhd", dscores, kgrp, preferred_element_type=jnp.float32).astype(
        jnp.bfloat16
    )
    gradk = jnp.einsum("rhk,rhd->kd", dscores, qgrp, preferred_element_type=jnp.float32)
    gradv = jnp.einsum("rhk,rhd->kd", probs_b, ggrp, preferred_element_type=jnp.float32)
    return (output, gradq, gradk, gradv)


def attend(queries, window, grad_out, allowed):
    rows = queries.shape[0]
    count = window.shape[0]
    group = HEADS // KV_HEADS
    kvw = KV_HEADS * HEAD
    qgrp = queries.reshape(rows, KV_HEADS, group, HEAD).transpose(1, 0, 2, 3)
    ggrp = grad_out.reshape(rows, KV_HEADS, group, HEAD).transpose(1, 0, 2, 3)
    kgrp = window[:, :kvw].reshape(count, KV_HEADS, HEAD).transpose(1, 0, 2)
    vgrp = window[:, kvw:].reshape(count, KV_HEADS, HEAD).transpose(1, 0, 2)
    output, gradq, gradk, gradv = lax.map(
        lambda ops: attend_group(ops, allowed), (qgrp, kgrp, vgrp, ggrp)
    )
    output = output.transpose(1, 0, 2, 3).reshape(rows, HEADS * HEAD)
    gradq = gradq.transpose(1, 0, 2, 3).reshape(rows, HEADS * HEAD)
    gradk = gradk.transpose(1, 0, 2).reshape(count, kvw)
    gradv = gradv.transpose(1, 0, 2).reshape(count, kvw)
    return (output, gradq, jnp.concatenate([gradk, gradv], axis=1))


def body(hidden, kv_blocks, kv_scale, queries, grad_out):
    tok = hidden.shape[0]
    groups = lax.axis_size("fsdp")
    reach = groups // 2
    place = lax.axis_index("fsdp")
    linear = lax.axis_index("seq") * groups + place
    weights = dequantize(kv_blocks, kv_scale)
    columns = lax.all_to_all(hidden, "fsdp", split_axis=1, concat_axis=0, tiled=True)
    rows = columns
    kv = lax.psum_scatter(
        jnp.dot(rows, weights, preferred_element_type=jnp.float32),
        "fsdp",
        scatter_dimension=0,
        tiled=True,
    ).astype(jnp.bfloat16)
    pieces = []
    for offset in range(reach, 0, -1):
        pieces.append(shifted(kv, ("seq", "fsdp"), offset))
    window = jnp.concatenate(pieces + [kv], axis=0)
    base = linear * tok
    qpos = base + jnp.arange(tok, dtype=jnp.int32)
    kpos = base - reach * tok + jnp.arange((reach + 1) * tok, dtype=jnp.int32)
    span = reach * tok
    allowed = (
        (qpos[:, None] - kpos[None, :] < span)
        & (kpos[None, :] <= qpos[:, None])
        & (kpos[None, :] >= 0)
    )
    attn_out, grad_queries, dwin = attend(queries, window, grad_out, allowed)
    total = dwin[reach * tok :]
    inside = total
    for offset in range(1, reach + 1):
        piece = dwin[(reach - offset) * tok : (reach - offset + 1) * tok]
        returned = shifted(piece, ("seq", "fsdp"), -offset)
        total = total + returned
        inside = inside + jnp.where(place + offset < groups, returned, jnp.zeros_like(returned))
    all_grad = total.astype(jnp.bfloat16)
    seg_grad = inside.astype(jnp.bfloat16)
    spread = lax.dot_general(
        lax.all_gather(seg_grad, "fsdp", axis=0, tiled=True),
        weights,
        (((1,), (1,)), ((), ())),
        preferred_element_type=jnp.float32,
    ).astype(jnp.bfloat16)
    grad_hidden = lax.all_to_all(spread, "fsdp", split_axis=0, concat_axis=1, tiled=True)
    rows = columns
    shard_grad = lax.dot_general(
        rows,
        lax.all_gather(all_grad, "fsdp", axis=0, tiled=True),
        (((0,), (0,)), ((), ())),
        preferred_element_type=jnp.float32,
    )
    weight_grad = lax.psum(shard_grad, "seq")
    return (attn_out, grad_queries, grad_hidden, weight_grad)


def solution(mesh):
    return jax.shard_map(
        body,
        mesh=mesh,
        in_specs=(
            P(("seq", "fsdp"), None),
            P("fsdp", None),
            P("fsdp", None),
            P(("seq", "fsdp"), None),
            P(("seq", "fsdp"), None),
        ),
        out_specs=(
            P(("seq", "fsdp"), None),
            P(("seq", "fsdp"), None),
            P(("seq", "fsdp"), None),
            P("fsdp", None),
        ),
        check_vma=False,
    )
```

profile of v0, /device:TPU:0, one launch (start us, length us, event | category | flops | bytes accessed | tf_op | source)
XLA Modules:
  0.0 503.2 jit_solution(12745964746301407682)
XLA Ops:
  7.2 4.1 copy.37
  11.2 6.5 %all-to-all-start = ((bf16[128,4,2048]{0,2,1:T(8,128)(2,1)}), bf16[128,4,2048]{0,2,1:T(8,128)(2,1)S(1)}, u32[]{:S(2)}, u32[]{:S(2)}) async-start(bf16[128,4,2048]{0,2,1:T(8,128)(2,1)} %bitcast.160), calls=%async_computation | async-start | bytes 4194304 | tf_op jit(solution)/shard_map/all_to_all | solution.py:74
  17.8 48.1 %all-to-all-done = bf16[128,4,2048]{0,2,1:T(8,128)(2,1)S(1)} async-done(((bf16[128,4,2048]{0,2,1:T(8,128)(2,1)}), bf16[128,4,2048]{0,2,1:T(8,128)(2,1)S(1)}, u32[]{:S(2)}, u32[]{:S(2)}) %all-to-all-start) | async-done | bytes 2097184 | tf_op jit(solution)/shard_map/all_to_all | solution.py:74
  69.1 4.2 copy-done
  74.4 4.0 convolution_bitcast_fusion.2
  78.5 42.8 %reduce-scatter.2.cloned.1.call-done = f32[128,1024]{0,1:T(8,128)} async-done(((f32[512,1024]{0,1:T(8,128)}), f32[128,1024]{0,1:T(8,128)}) %reduce-scatter.2.cloned.1.call-update) | async-done | bytes 524304 | tf_op jit(solution)/shard_map/reduce_scatter | solution.py:76
  125.0 4.3 collective-permute-start
  137.0 110.8 %while.17 = (s32[]{:T(128)}, bf16[4,128,8,128]{3,1,2,0:T(8,128)(2,1)}, bf16[4,128,8,128]{3,1,2,0:T(8,128)(2,1)}, f32[4,384,128]{1,2,0:T(8,128)S(1)}, f32[4,384,1...) while((s32[]{:T(128)}, ...), condition=%wide.region_5.6_spmd.clone, body=%wide.region_1.5_spmd.clone.sunk | while | flops 816830336 | bytes 25336436 | solution.py:57
  145.2 8.0 %fusion.155 = bf16[4,128,8,128]{3,1,2,0:T(8,128)(2,1)} fusion(bf16[4,128,8,128]{3,1,2,0:T(8,128)(2,1)} %get-tuple-element.254, s32[]{:T(128)S(6)} %copy.76, f32[128,8,384]{2,0,1:T(8,128)S(1)} %fusion.154, bf16[4,384,128]{2,1,0:T(8,128)(2,1)} %copy-done.9, f32[128,8,384]{2,0,1:T(8,128)} %get-tuple-element.238, f32[128,8]{0,1:T(8,128)S(1)} %get-tuple-element.237), kind=kOutput, calls=%fused_computation.16.clone.1 | convolution fusion | flops 103548288 | bytes 6661120 | tf_op jit(solution)/shard_map/while/body/eval_jaxpr/rhk,kd->rhd/dot_general | solution.py:40
  153.2 7.5 %fusion.156 = f32[4,384,128]{1,2,0:T(8,128)S(1)} fusion(f32[4,384,128]{1,2,0:T(8,128)S(1)} %get-tuple-element.255, s32[]{:T(128)S(6)} %copy.76, f32[128,8,384]{2,0,1:T(8,128)S(1)} %fusion.154, bf16[4,128,8,128]{1,3,2,0:T(8,128)(2,1)} %get-tuple-element.270, f32[128,8,384]{2,0,1:T(8,128)} %get-tuple-element.238, f32[128,8]{0,1:T(8,128)S(1)} %get-tuple-element.237), kind=kOutput, calls=%fused_computation.20.clone.1 | convolution fusion | flops 103417216 | bytes 6759424 | tf_op jit(solution)/shard_map/while/body/eval_jaxpr/rhk,rhd->kd/dot_general | solution.py:43
  172.9 8.0 %fusion.155 = bf16[4,128,8,128]{3,1,2,0:T(8,128)(2,1)} fusion(bf16[4,128,8,128]{3,1,2,0:T(8,128)(2,1)} %get-tuple-element.254, s32[]{:T(128)S(6)} %copy.76, f32[128,8,384]{2,0,1:T(8,128)S(1)} %fusion.154, bf16[4,384,128]{2,1,0:T(8,128)(2,1)} %copy-done.9, f32[128,8,384]{2,0,1:T(8,128)} %get-tuple-element.238, f32[128,8]{0,1:T(8,128)S(1)} %get-tuple-element.237), kind=kOutput, calls=%fused_computation.16.clone.1 | convolution fusion | flops 103548288 | bytes 6661120 | tf_op jit(solution)/shard_map/while/body/eval_jaxpr/rhk,kd->rhd/dot_general | solution.py:40
  180.9 7.5 %fusion.156 = f32[4,384,128]{1,2,0:T(8,128)S(1)} fusion(f32[4,384,128]{1,2,0:T(8,128)S(1)} %get-tuple-element.255, s32[]{:T(128)S(6)} %copy.76, f32[128,8,384]{2,0,1:T(8,128)S(1)} %fusion.154, bf16[4,128,8,128]{1,3,2,0:T(8,128)(2,1)} %get-tuple-element.270, f32[128,8,384]{2,0,1:T(8,128)} %get-tuple-element.238, f32[128,8]{0,1:T(8,128)S(1)} %get-tuple-element.237), kind=kOutput, calls=%fused_computation.20.clone.1 | convolution fusion | flops 103417216 | bytes 6759424 | tf_op jit(solution)/shard_map/while/body/eval_jaxpr/rhk,rhd->kd/dot_general | solution.py:43
  200.6 8.0 %fusion.155 = bf16[4,128,8,128]{3,1,2,0:T(8,128)(2,1)} fusion(bf16[4,128,8,128]{3,1,2,0:T(8,128)(2,1)} %get-tuple-element.254, s32[]{:T(128)S(6)} %copy.76, f32[128,8,384]{2,0,1:T(8,128)S(1)} %fusion.154, bf16[4,384,128]{2,1,0:T(8,128)(2,1)} %copy-done.9, f32[128,8,384]{2,0,1:T(8,128)} %get-tuple-element.238, f32[128,8]{0,1:T(8,128)S(1)} %get-tuple-element.237), kind=kOutput, calls=%fused_computation.16.clone.1 | convolution fusion | flops 103548288 | bytes 6661120 | tf_op jit(solution)/shard_map/while/body/eval_jaxpr/rhk,kd->rhd/dot_general | solution.py:40
  208.5 7.5 %fusion.156 = f32[4,384,128]{1,2,0:T(8,128)S(1)} fusion(f32[4,384,128]{1,2,0:T(8,128)S(1)} %get-tuple-element.255, s32[]{:T(128)S(6)} %copy.76, f32[128,8,384]{2,0,1:T(8,128)S(1)} %fusion.154, bf16[4,128,8,128]{1,3,2,0:T(8,128)(2,1)} %get-tuple-element.270, f32[128,8,384]{2,0,1:T(8,128)} %get-tuple-element.238, f32[128,8]{0,1:T(8,128)S(1)} %get-tuple-element.237), kind=kOutput, calls=%fused_computation.20.clone.1 | convolution fusion | flops 103417216 | bytes 6759424 | tf_op jit(solution)/shard_map/while/body/eval_jaxpr/rhk,rhd->kd/dot_general | solution.py:43
  228.3 8.0 %fusion.155 = bf16[4,128,8,128]{3,1,2,0:T(8,128)(2,1)} fusion(bf16[4,128,8,128]{3,1,2,0:T(8,128)(2,1)} %get-tuple-element.254, s32[]{:T(128)S(6)} %copy.76, f32[128,8,384]{2,0,1:T(8,128)S(1)} %fusion.154, bf16[4,384,128]{2,1,0:T(8,128)(2,1)} %copy-done.9, f32[128,8,384]{2,0,1:T(8,128)} %get-tuple-element.238, f32[128,8]{0,1:T(8,128)S(1)} %get-tuple-element.237), kind=kOutput, calls=%fused_computation.16.clone.1 | convolution fusion | flops 103548288 | bytes 6661120 | tf_op jit(solution)/shard_map/while/body/eval_jaxpr/rhk,kd->rhd/dot_general | solution.py:40
  236.2 7.5 %fusion.156 = f32[4,384,128]{1,2,0:T(8,128)S(1)} fusion(f32[4,384,128]{1,2,0:T(8,128)S(1)} %get-tuple-element.255, s32[]{:T(128)S(6)} %copy.76, f32[128,8,384]{2,0,1:T(8,128)S(1)} %fusion.154, bf16[4,128,8,128]{1,3,2,0:T(8,128)(2,1)} %get-tuple-element.270, f32[128,8,384]{2,0,1:T(8,128)} %get-tuple-element.238, f32[128,8]{0,1:T(8,128)S(1)} %get-tuple-element.237), kind=kOutput, calls=%fused_computation.20.clone.1 | convolution fusion | flops 103417216 | bytes 6759424 | tf_op jit(solution)/shard_map/while/body/eval_jaxpr/rhk,rhd->kd/dot_general | solution.py:43
  252.3 32.5 %collective-permute-done.3 = f32[128,1024]{0,1:T(8,128)} collective-permute-done((f32[128,1024]{0,1:T(8,128)}, f32[128,1024]{0,1:T(8,128)}, u32[]{:S(2)}, u32[]{:S(2)}) %collective-permute-start.3) | collective-permute-done | bytes 524320 | tf_op jit(solution)/shard_map/ppermute | solution.py:16
  288.2 41.5 %all-gather.5.cloned.1.call-done = bf16[512,1024]{0,1:T(8,128)(2,1)} async-done(((bf16[128,1024]{0,1:T(8,128)(2,1)}), bf16[512,1024]{0,1:T(8,128)(2,1)}) %all-gather.5.cloned.1.call-update) | async-done | bytes 1048592 | tf_op jit(solution)/shard_map/all_gather | solution.py:115
  329.7 6.8 %convolution_bitcast_fusion.1 = f32[2048,1024]{0,1:T(8,128)} fusion(bf16[512,1024]{0,1:T(8,128)(2,1)} %all-gather.5.cloned.1.call-done, bf16[512,2048]{1,0:T(8,128)(2,1)S(1)} %bitcast.162), kind=kOutput, calls=%fused_computation.64 | convolution fusion | flops 2147483648 | bytes 11534336 | tf_op jit(solution)/shard_map/dot_general | solution.py:113
  336.5 23.0 %all-gather.3.cloned.1.call-done = bf16[512,1024]{0,1:T(8,128)(2,1)} async-done(((bf16[128,1024]{0,1:T(8,128)(2,1)}), bf16[512,1024]{0,1:T(8,128)(2,1)}) %all-gather.3.cloned.1.call-update) | async-done | bytes 1048592 | tf_op jit(solution)/shard_map/all_gather | solution.py:106
  359.6 9.0 %convolution_convert_fusion.1 = bf16[512,2048]{1,0:T(8,128)(2,1)} fusion(bf16[512,1024]{0,1:T(8,128)(2,1)} %all-gather.3.cloned.1.call-done, f32[256,8,8,128]{3,2,1,0:T(8,128)} %bitcast.157, bf16[2048,1024]{1,0:T(8,128)(2,1)} %param.8), kind=kOutput, calls=%fused_computation.65 | convolution fusion | flops 2154823680 | bytes 15728640 | tf_op jit(solution)/shard_map/dot_general | solution.py:105
  376.7 42.7 %all-to-all-done.1 = bf16[4,128,2048]{2,1,0:T(8,128)(2,1)S(1)} async-done(((bf16[4,128,2048]{2,1,0:T(8,128)(2,1)}), bf16[4,128,2048]{2,1,0:T(8,128)(2,1)S(1)}, u32[]{:S(2)}, u32[]{:S(2)}) %all-to-all-start.1) | async-done | bytes 2097184 | tf_op jit(solution)/shard_map/all_to_all | solution.py:111
  420.9 66.5 %all-reduce.2.cloned.1.call-done = f32[2048,1024]{0,1:T(8,128)} async-done(((f32[2048,1024]{0,1:T(8,128)}), f32[2048,1024]{0,1:T(8,128)}) %all-reduce.2.cloned.1.call-update) | async-done | bytes 8388624 | tf_op jit(solution)/shard_map/psum | solution.py:119
  487.4 9.2 %copy.49 = f32[2048,1024]{1,0:T(8,128)} copy(f32[2048,1024]{0,1:T(8,128)} %all-reduce.2.cloned.1.call-done) | data formatting | bytes 16777216
  (105 shorter events, 81.7 us)
Async XLA Ops:
  11.2 6.5 %copy-start.11 = (f32[16,8]{0,1:T(8,128)S(1)}, f32[16,8]{0,1:T(8,128)}, u32[]{:S(2)}) copy-start(f32[16,8]{0,1:T(8,128)} %param.9) | copy-start | bytes 1540
  11.2 54.7 %all-to-all-start = ((bf16[128,4,2048]{0,2,1:T(8,128)(2,1)}), bf16[128,4,2048]{0,2,1:T(8,128)(2,1)S(1)}, u32[]{:S(2)}, u32[]{:S(2)}) async-start(bf16[128,4,2048]{0,2,1:T(8,128)(2,1)} %bitcast.160), calls=%async_computation | async-start | bytes 4194304 | tf_op jit(solution)/shard_map/all_to_all | solution.py:74
  17.7 103.6 %reduce-scatter.2.cloned.1.call-start = ((), (), s32[]{:S(2)}) async-start(), calls=%async_computation.3 | async-start | bytes 2621440 | tf_op jit(solution)/shard_map/reduce_scatter | solution.py:76
  68.5 4.9 copy-start.1
  68.5 5.9 %copy-start.2 = (bf16[4,128,2048]{2,1,0:T(8,128)(2,1)S(1)}, bf16[4,128,2048]{2,1,0:T(8,128)(2,1)}, u32[]{:S(2)}) copy-start(bf16[4,128,2048]{2,1,0:T(8,128)(2,1)} %copy.38) | copy-start | bytes 6291460
  69.1 4.3 copy-start
  78.4 50.9 %copy-start.6 = (bf16[128,4096]{1,0:T(8,128)(2,1)S(1)}, bf16[128,4096]{1,0:T(8,128)(2,1)}, u32[]{:S(2)}) copy-start(bf16[128,4096]{1,0:T(8,128)(2,1)} %param.10) | copy-start | bytes 3145732
  78.4 251.3 %all-gather.5.cloned.1.call-start = ((), (), s32[]{:S(2)}) async-start(), calls=%async_computation.5 | async-start | bytes 1310720 | tf_op jit(solution)/shard_map/all_gather | solution.py:115
  122.4 9.8 %collective-permute-start.1 = (bf16[128,1024]{0,1:T(8,128)(2,1)S(1)}, bf16[128,1024]{0,1:T(8,128)(2,1)S(1)}, u32[]{:S(2)}, u32[]{:S(2)}) collective-permute-start(bf16[128,1024]{0,1:T(8,128)(2,1)S(1)} %convert_element_type.32), channel_id=1, source_target_pairs={{0,1},{1,2},{2,3},{3,4},{4,5},{5,6},{6,7},{7,8},{8,9},{9,10},{10,1... | collective-permute-start | bytes 786440 | tf_op jit(solution)/shard_map/ppermute | solution.py:16
  125.0 10.4 %collective-permute-start = (bf16[128,1024]{0,1:T(8,128)(2,1)S(1)}, bf16[128,1024]{0,1:T(8,128)(2,1)}, u32[]{:S(2)}, u32[]{:S(2)}) collective-permute-start(bf16[128,1024]{0,1:T(8,128)(2,1)S(1)} %convert_element_type.32), channel_id=1, source_target_pairs={{0,2},{1,3},{2,4},{3,5},{4,6},{5,7},{6,8},{7,9},{8,10},{9,11},{10,... | collective-permute-start | bytes 786440 | tf_op jit(solution)/shard_map/ppermute | solution.py:16
  137.0 6.9 %copy-start.4 = (bf16[4,384,128]{2,1,0:T(8,128)(2,1)}, bf16[4,384,128]{2,1,0:T(8,128)(2,1)S(1)}, u32[]{:S(2)}) copy-start(bf16[4,384,128]{2,1,0:T(8,128)(2,1)S(1)} %get-tuple-element.272) | copy-start | bytes 1179652 | tf_op jit(solution)/shard_map/while
  137.1 6.9 %copy-start.9 = (bf16[4,384,128]{2,1,0:T(8,128)(2,1)}, bf16[4,384,128]{2,1,0:T(8,128)(2,1)S(1)}, u32[]{:S(2)}) copy-start(bf16[4,384,128]{2,1,0:T(8,128)(2,1)S(1)} %get-tuple-element.271) | copy-start | bytes 1179652 | tf_op jit(solution)/shard_map/while
  164.7 6.9 %copy-start.4 = (bf16[4,384,128]{2,1,0:T(8,128)(2,1)}, bf16[4,384,128]{2,1,0:T(8,128)(2,1)S(1)}, u32[]{:S(2)}) copy-start(bf16[4,384,128]{2,1,0:T(8,128)(2,1)S(1)} %get-tuple-element.272) | copy-start | bytes 1179652 | tf_op jit(solution)/shard_map/while
  164.7 6.9 %copy-start.9 = (bf16[4,384,128]{2,1,0:T(8,128)(2,1)}, bf16[4,384,128]{2,1,0:T(8,128)(2,1)S(1)}, u32[]{:S(2)}) copy-start(bf16[4,384,128]{2,1,0:T(8,128)(2,1)S(1)} %get-tuple-element.271) | copy-start | bytes 1179652 | tf_op jit(solution)/shard_map/while
  192.4 6.9 %copy-start.4 = (bf16[4,384,128]{2,1,0:T(8,128)(2,1)}, bf16[4,384,128]{2,1,0:T(8,128)(2,1)S(1)}, u32[]{:S(2)}) copy-start(bf16[4,384,128]{2,1,0:T(8,128)(2,1)S(1)} %get-tuple-element.272) | copy-start | bytes 1179652 | tf_op jit(solution)/shard_map/while
  192.4 6.9 %copy-start.9 = (bf16[4,384,128]{2,1,0:T(8,128)(2,1)}, bf16[4,384,128]{2,1,0:T(8,128)(2,1)S(1)}, u32[]{:S(2)}) copy-start(bf16[4,384,128]{2,1,0:T(8,128)(2,1)S(1)} %get-tuple-element.271) | copy-start | bytes 1179652 | tf_op jit(solution)/shard_map/while
  220.1 6.9 %copy-start.4 = (bf16[4,384,128]{2,1,0:T(8,128)(2,1)}, bf16[4,384,128]{2,1,0:T(8,128)(2,1)S(1)}, u32[]{:S(2)}) copy-start(bf16[4,384,128]{2,1,0:T(8,128)(2,1)S(1)} %get-tuple-element.272) | copy-start | bytes 1179652 | tf_op jit(solution)/shard_map/while
  220.1 6.9 %copy-start.9 = (bf16[4,384,128]{2,1,0:T(8,128)(2,1)}, bf16[4,384,128]{2,1,0:T(8,128)(2,1)S(1)}, u32[]{:S(2)}) copy-start(bf16[4,384,128]{2,1,0:T(8,128)(2,1)S(1)} %get-tuple-element.271) | copy-start | bytes 1179652 | tf_op jit(solution)/shard_map/while
  249.7 35.1 %collective-permute-start.3 = (f32[128,1024]{0,1:T(8,128)}, f32[128,1024]{0,1:T(8,128)}, u32[]{:S(2)}, u32[]{:S(2)}) collective-permute-start(f32[128,1024]{0,1:T(8,128)} %get-tuple-element.157), channel_id=1, source_target_pairs={{2,0},{3,1},{4,2},{5,3},{6,4},{7,5},{8,6},{9,7},{10,8},{11,9},{12,... | collective-permute-start | bytes 1572872 | tf_op jit(solution)/shard_map/ppermute | solution.py:16
  251.0 33.8 %collective-permute-start.2 = (f32[128,1024]{0,1:T(8,128)S(1)}, f32[128,1024]{0,1:T(8,128)}, u32[]{:S(2)}, u32[]{:S(2)}) collective-permute-start(f32[128,1024]{0,1:T(8,128)S(1)} %get-tuple-element.156), channel_id=1, source_target_pairs={{1,0},{2,1},{3,2},{4,3},{5,4},{6,5},{7,6},{8,7},{9,8},{10,9},{11,1... | collective-permute-start | bytes 1572872 | tf_op jit(solution)/shard_map/ppermute | solution.py:16
  252.3 77.4 %copy-start.3 = (bf16[4,128,2048]{2,1,0:T(8,128)(2,1)S(1)}, bf16[4,128,2048]{2,1,0:T(8,128)(2,1)}, u32[]{:S(2)}) copy-start(bf16[4,128,2048]{2,1,0:T(8,128)(2,1)} %copy.38) | copy-start | bytes 6291460
  287.2 72.4 %all-gather.3.cloned.1.call-start = ((), (), s32[]{:S(2)}) async-start(), calls=%async_computation.4 | async-start | bytes 1310720 | tf_op jit(solution)/shard_map/all_gather | solution.py:106
  288.0 199.5 %all-reduce.2.cloned.1.call-start = ((), (), s32[]{:S(2)}) async-start(), calls=%async_computation.6 | async-start | bytes 16777216 | tf_op jit(solution)/shard_map/psum | solution.py:119
  368.6 50.8 %all-to-all-start.1 = ((bf16[4,128,2048]{2,1,0:T(8,128)(2,1)}), bf16[4,128,2048]{2,1,0:T(8,128)(2,1)S(1)}, u32[]{:S(2)}, u32[]{:S(2)}) async-start(bf16[4,128,2048]{2,1,0:T(8,128)(2,1)} %bitcast.18), calls=%async_computation.2 | async-start | bytes 4194304 | tf_op jit(solution)/shard_map/all_to_all | solution.py:111
  (10 other events, 37.2 us)
Sparse Core Ops, SparseCore 0:
  78.6 42.7 reduce-scatter.1
  287.3 42.3 all-gather.4
  331.3 28.2 all-gather.2
  362.9 124.4 all-reduce.1
where the time goes:
time: 504 us; the launch traced here: 503 us
  waiting for transfers between devices  301 us (60%)
  matrix products  130 us (26%)
  local copies, waits for them, and re-layouts  31 us (6%)
  starting transfers between devices  20.2 us (4%)
  between operations  13.9 us (3%)
  other arithmetic  6.91 us (1%)
    psum x1, waiting for transfers between devices, body(): weight_grad = lax.psum(shard_grad, 'seq')  66.5 us
    all_to_all x1, waiting for transfers between devices, body(): lax.all_to_all(hidden, 'fsdp', split_axis=1, concat_axis=0, tiled=True)  48.1 us
    reduce_scatter x1, waiting for transfers between devices, body(): lax.psum_scatter(jnp.dot(rows, weights, preferred_element_type=jnp.float3...  42.8 us
    all_to_all x1, waiting for transfers between devices, body(): lax.all_to_all(spread, 'fsdp', split_axis=0, concat_axis=1, tiled=True)  42.7 us
    all_gather x1, waiting for transfers between devices, body(): lax.all_gather(all_grad, 'fsdp', axis=0, tiled=True)  41.5 us
    ppermute x4, waiting for transfers between devices, shifted(): return lax.ppermute(block, axis, route)  35.6 us
    dot_general x4, matrix products, attend_group(): jnp.einsum('rhk,kd->rhd', dscores, kgrp, preferred_element_type=jnp.float32)  31.9 us
    dot_general x4, matrix products, attend_group(): jnp.einsum('rhk,rhd->kd', dscores, qgrp, preferred_element_type=jnp.float32)  30 us
  transfers between devices with their start and end apart: 10, of which 8 were waited for; matrix products, arithmetic and copies ran while one was open for 5% of the time, Pallas kernels for 0%

commit v1 on v0

--- a/solution.py
+++ b/solution.py
@@ -8,6 +8,18 @@
 HEAD = 128
 QB = 128
 NEG = -1e30
+
+
+def cut_along(array, dim, count):
+    lengths = array.shape
+    parts = array.reshape(*lengths[:dim], count, lengths[dim] // count, *lengths[dim + 1 :])
+    return jnp.moveaxis(parts, dim, 0)
+
+
+def in_order(pieces, dim):
+    pieces = jnp.moveaxis(pieces, 0, dim)
+    shape = pieces.shape
+    return pieces.reshape(*shape[:dim], shape[dim] * shape[dim + 1], *shape[dim + 2 :])
 
 
 def shifted(block, axis, distance):
@@ -71,7 +83,14 @@
     place = lax.axis_index("fsdp")
     linear = lax.axis_index("seq") * groups + place
     weights = dequantize(kv_blocks, kv_scale)
-    columns = lax.all_to_all(hidden, "fsdp", split_axis=1, concat_axis=0, tiled=True)
+    size, index = (lax.axis_size("fsdp"), lax.axis_index("fsdp"))
+    tiles = cut_along(hidden, 1, size)
+    done = [tiles[index]]
+    for lap in range(1, size):
+        sent = tiles[index ^ lap]
+        done.append(lax.ppermute(sent, "fsdp", [(i_2, i_2 ^ lap) for i_2 in range(size)]))
+    tiles = jnp.stack(done)[index ^ jnp.arange(size)]
+    columns = in_order(tiles, 0)
     rows = columns
     kv = lax.psum_scatter(
         jnp.dot(rows, weights, preferred_element_type=jnp.float32),

time: 504 us -> 505 us (level)
  local copies, waits for them, and re-layouts: 31 us -> 36.6 us
    all_to_all x1 -> x0, waiting for transfers between devices: 48.1 us -> none  [body(): lax.all_to_all(hidden, 'fsdp', split_axis=1, concat_axis=0, tiled=True)]
    ppermute x0 -> x3, waiting for transfers between devices: none -> 42.4 us  [body(): lax.ppermute(sent, 'fsdp', [(i_2, i_2 ^ lap) for i_2 in range(size)])]
    all_to_all x1 -> x0, starting transfers between devices: 6.48 us -> none  [body(): lax.all_to_all(hidden, 'fsdp', split_axis=1, concat_axis=0, tiled=True)]
    ppermute x0 -> x3, starting transfers between devices: none -> 5.84 us  [body(): lax.ppermute(sent, 'fsdp', [(i_2, i_2 ^ lap) for i_2 in range(size)])]
    unnamed x21 -> x32, local copies, waits for them, and re-layouts: 22.2 us -> 22.3 us
  transfers between devices with their start and end apart: 10 -> 12, of which waited for: 8 -> 9; matrix products, arithmetic and copies ran while one was open for 5% -> 5% of each run, Pallas kernels for 0% -> 0%
where the time goes in v1:
time: 505 us; the launch traced here: 503 us
  waiting for transfers between devices  297 us (59%)
  matrix products  127 us (25%)
  local copies, waits for them, and re-layouts  36.6 us (7%)
  starting transfers between devices  19.6 us (4%)
  between operations  14 us (3%)
  other arithmetic  8.94 us (2%)
    psum x1, waiting for transfers between devices, body(): weight_grad = lax.psum(shard_grad, 'seq')  66.5 us
    reduce_scatter x1, waiting for transfers between devices, body(): lax.psum_scatter(jnp.dot(rows, weights, preferred_element_type=jnp.float3...  43.8 us
    all_to_all x1, waiting for transfers between devices, body(): lax.all_to_all(spread, 'fsdp', split_axis=0, concat_axis=1, tiled=True)  42.7 us
    ppermute x3, waiting for transfers between devices, body(): lax.ppermute(sent, 'fsdp', [(i_2, i_2 ^ lap) for i_2 in range(size)])  42.4 us
    all_gather x1, waiting for transfers between devices, body(): lax.all_gather(all_grad, 'fsdp', axis=0, tiled=True)  41.4 us
    ppermute x4, waiting for transfers between devices, shifted(): return lax.ppermute(block, axis, route)  36.7 us
    dot_general x4, matrix products, attend_group(): jnp.einsum('rhk,kd->rhd', dscores, kgrp, preferred_element_type=jnp.float32)  31.8 us
    dot_general x4, matrix products, attend_group(): jnp.einsum('rhk,rhd->kd', dscores, qgrp, preferred_element_type=jnp.float32)  30 us
  transfers between devices with their start and end apart: 12, of which 9 were waited for; matrix products, arithmetic and copies ran while one was open for 5% of the time, Pallas kernels for 0%

profile of v1, /device:TPU:0, one launch (start us, length us, event | category | flops | bytes accessed | tf_op | source)
XLA Modules:
  0.0 503.5 jit_solution(8354212331299904511)
XLA Ops:
  12.8 5.1 %collective-permute-start.2 = (bf16[128,2048]{1,0:T(8,128)(2,1)S(1)}, bf16[128,2048]{1,0:T(8,128)(2,1)S(1)}, u32[]{:S(2)}, u32[]{:S(2)}) collective-permute-start(bf16[128,2048]{1,0:T(8,128)(2,1)S(1)} %bitcast.190), channel_id=1, source_target_pairs={{0,3},{1,2},{2,1},{3,0},{4,7},{5,6},{6,5},{7,4},{8,11},{9,10},{10,... | collective-permute-start | bytes 1572872 | tf_op jit(solution)/shard_map/ppermute | solution.py:91
  20.5 10.4 %collective-permute-done.2 = bf16[128,2048]{1,0:T(8,128)(2,1)S(1)} collective-permute-done((bf16[128,2048]{1,0:T(8,128)(2,1)S(1)}, bf16[128,2048]{1,0:T(8,128)(2,1)S(1)}, u32[]{:S(2)}, u32[]{:S(2)}) %collective-permute-start.2) | collective-permute-done | bytes 524320 | tf_op jit(solution)/shard_map/ppermute | solution.py:91
  30.9 32.0 %collective-permute-done.1 = bf16[128,2048]{1,0:T(8,128)(2,1)} collective-permute-done((bf16[128,2048]{1,0:T(8,128)(2,1)S(1)}, bf16[128,2048]{1,0:T(8,128)(2,1)}, u32[]{:S(2)}, u32[]{:S(2)}) %collective-permute-start.1) | collective-permute-done | bytes 524320 | tf_op jit(solution)/shard_map/ppermute | solution.py:91
  67.1 4.2 copy-done
  76.5 43.8 %reduce-scatter.2.cloned.1.call-done = f32[128,1024]{1,0:T(8,128)} async-done(((f32[512,1024]{1,0:T(8,128)}), f32[128,1024]{1,0:T(8,128)}) %reduce-scatter.2.cloned.1.call-update) | async-done | bytes 524304 | tf_op jit(solution)/shard_map/reduce_scatter | solution.py:95
  124.0 4.3 collective-permute-start.3
  130.3 4.1 collective-permute-done.3
  136.8 111.6 %while.17 = (s32[]{:T(128)}, bf16[4,128,8,128]{3,1,2,0:T(8,128)(2,1)S(1)}, bf16[4,128,8,128]{3,1,2,0:T(8,128)(2,1)}, f32[4,384,128]{1,2,0:T(8,128)S(1)}, f32[4,3...) while((s32[]{:T(128)}, ...), condition=%wide.region_5.6_spmd.clone, body=%wide.region_1.5_spmd.clone.sunk | while | flops 816830336 | bytes 30579316 | solution.py:69
  145.1 8.0 %fusion.157 = bf16[4,128,8,128]{3,1,2,0:T(8,128)(2,1)} fusion(bf16[4,128,8,128]{3,1,2,0:T(8,128)(2,1)} %get-tuple-element.246, s32[]{:T(128)S(6)} %copy.82, f32[128,8,384]{2,0,1:T(8,128)S(1)} %fusion.156, bf16[4,384,128]{2,1,0:T(8,128)(2,1)} %get-tuple-element.263, f32[128,8,384]{2,0,1:T(8,128)} %get-tuple-element.230, ...), kind=kOutput, calls=%fused_computation.17.clone.1 | convolution fusion | flops 103548288 | bytes 6661120 | tf_op jit(solution)/shard_map/while/body/eval_jaxpr/rhk,kd->rhd/dot_general | solution.py:52
  153.1 7.5 %fusion.158 = f32[4,384,128]{1,2,0:T(8,128)S(1)} fusion(f32[4,384,128]{1,2,0:T(8,128)S(1)} %get-tuple-element.247, s32[]{:T(128)S(6)} %copy.82, f32[128,8,384]{2,0,1:T(8,128)S(1)} %fusion.156, bf16[4,128,8,128]{1,3,2,0:T(8,128)(2,1)} %get-tuple-element.262, f32[128,8,384]{2,0,1:T(8,128)} %get-tuple-element.230, f32[128,8]{0,1:T(8,128)S(1)} %get-tuple-element.229), kind=kOutput, calls=%fused_computation.21.clone.1 | convolution fusion | flops 103417216 | bytes 6759424 | tf_op jit(solution)/shard_map/while/body/eval_jaxpr/rhk,rhd->kd/dot_general | solution.py:55
  173.1 7.9 %fusion.157 = bf16[4,128,8,128]{3,1,2,0:T(8,128)(2,1)} fusion(bf16[4,128,8,128]{3,1,2,0:T(8,128)(2,1)} %get-tuple-element.246, s32[]{:T(128)S(6)} %copy.82, f32[128,8,384]{2,0,1:T(8,128)S(1)} %fusion.156, bf16[4,384,128]{2,1,0:T(8,128)(2,1)} %get-tuple-element.263, f32[128,8,384]{2,0,1:T(8,128)} %get-tuple-element.230, ...), kind=kOutput, calls=%fused_computation.17.clone.1 | convolution fusion | flops 103548288 | bytes 6661120 | tf_op jit(solution)/shard_map/while/body/eval_jaxpr/rhk,kd->rhd/dot_general | solution.py:52
  181.0 7.5 %fusion.158 = f32[4,384,128]{1,2,0:T(8,128)S(1)} fusion(f32[4,384,128]{1,2,0:T(8,128)S(1)} %get-tuple-element.247, s32[]{:T(128)S(6)} %copy.82, f32[128,8,384]{2,0,1:T(8,128)S(1)} %fusion.156, bf16[4,128,8,128]{1,3,2,0:T(8,128)(2,1)} %get-tuple-element.262, f32[128,8,384]{2,0,1:T(8,128)} %get-tuple-element.230, f32[128,8]{0,1:T(8,128)S(1)} %get-tuple-element.229), kind=kOutput, calls=%fused_computation.21.clone.1 | convolution fusion | flops 103417216 | bytes 6759424 | tf_op jit(solution)/shard_map/while/body/eval_jaxpr/rhk,rhd->kd/dot_general | solution.py:55
  201.0 7.9 %fusion.157 = bf16[4,128,8,128]{3,1,2,0:T(8,128)(2,1)} fusion(bf16[4,128,8,128]{3,1,2,0:T(8,128)(2,1)} %get-tuple-element.246, s32[]{:T(128)S(6)} %copy.82, f32[128,8,384]{2,0,1:T(8,128)S(1)} %fusion.156, bf16[4,384,128]{2,1,0:T(8,128)(2,1)} %get-tuple-element.263, f32[128,8,384]{2,0,1:T(8,128)} %get-tuple-element.230, ...), kind=kOutput, calls=%fused_computation.17.clone.1 | convolution fusion | flops 103548288 | bytes 6661120 | tf_op jit(solution)/shard_map/while/body/eval_jaxpr/rhk,kd->rhd/dot_general | solution.py:52
  209.0 7.5 %fusion.158 = f32[4,384,128]{1,2,0:T(8,128)S(1)} fusion(f32[4,384,128]{1,2,0:T(8,128)S(1)} %get-tuple-element.247, s32[]{:T(128)S(6)} %copy.82, f32[128,8,384]{2,0,1:T(8,128)S(1)} %fusion.156, bf16[4,128,8,128]{1,3,2,0:T(8,128)(2,1)} %get-tuple-element.262, f32[128,8,384]{2,0,1:T(8,128)} %get-tuple-element.230, f32[128,8]{0,1:T(8,128)S(1)} %get-tuple-element.229), kind=kOutput, calls=%fused_computation.21.clone.1 | convolution fusion | flops 103417216 | bytes 6759424 | tf_op jit(solution)/shard_map/while/body/eval_jaxpr/rhk,rhd->kd/dot_general | solution.py:55
  228.9 7.9 %fusion.157 = bf16[4,128,8,128]{3,1,2,0:T(8,128)(2,1)} fusion(bf16[4,128,8,128]{3,1,2,0:T(8,128)(2,1)} %get-tuple-element.246, s32[]{:T(128)S(6)} %copy.82, f32[128,8,384]{2,0,1:T(8,128)S(1)} %fusion.156, bf16[4,384,128]{2,1,0:T(8,128)(2,1)} %get-tuple-element.263, f32[128,8,384]{2,0,1:T(8,128)} %get-tuple-element.230, ...), kind=kOutput, calls=%fused_computation.17.clone.1 | convolution fusion | flops 103548288 | bytes 6661120 | tf_op jit(solution)/shard_map/while/body/eval_jaxpr/rhk,kd->rhd/dot_general | solution.py:52
  236.8 7.5 %fusion.158 = f32[4,384,128]{1,2,0:T(8,128)S(1)} fusion(f32[4,384,128]{1,2,0:T(8,128)S(1)} %get-tuple-element.247, s32[]{:T(128)S(6)} %copy.82, f32[128,8,384]{2,0,1:T(8,128)S(1)} %fusion.156, bf16[4,128,8,128]{1,3,2,0:T(8,128)(2,1)} %get-tuple-element.262, f32[128,8,384]{2,0,1:T(8,128)} %get-tuple-element.230, f32[128,8]{0,1:T(8,128)S(1)} %get-tuple-element.229), kind=kOutput, calls=%fused_computation.21.clone.1 | convolution fusion | flops 103417216 | bytes 6759424 | tf_op jit(solution)/shard_map/while/body/eval_jaxpr/rhk,rhd->kd/dot_general | solution.py:55
  253.5 32.6 %collective-permute-done.6 = f32[128,1024]{0,1:T(8,128)} collective-permute-done((f32[128,1024]{0,1:T(8,128)}, f32[128,1024]{0,1:T(8,128)}, u32[]{:S(2)}, u32[]{:S(2)}) %collective-permute-start.6) | collective-permute-done | bytes 524320 | tf_op jit(solution)/shard_map/ppermute | solution.py:28
  289.4 41.4 %all-gather.5.cloned.1.call-done = bf16[512,1024]{0,1:T(8,128)(2,1)} async-done(((bf16[128,1024]{0,1:T(8,128)(2,1)}), bf16[512,1024]{0,1:T(8,128)(2,1)}) %all-gather.5.cloned.1.call-update) | async-done | bytes 1048592 | tf_op jit(solution)/shard_map/all_gather | solution.py:134
  330.8 6.9 %fusion.109 = f32[2048,1024]{1,0:T(8,128)} fusion(bf16[512,2048]{1,0:T(8,128)(2,1)S(1)} %bitcast.175, bf16[512,1024]{0,1:T(8,128)(2,1)} %all-gather.5.cloned.1.call-done), kind=kOutput, calls=%fused_computation.95 | convolution fusion | flops 2147483648 | bytes 11534336 | tf_op jit(solution)/shard_map/dot_general | solution.py:132
  337.7 22.9 %all-gather.3.cloned.1.call-done = bf16[512,1024]{0,1:T(8,128)(2,1)} async-done(((bf16[128,1024]{0,1:T(8,128)(2,1)}), bf16[512,1024]{0,1:T(8,128)(2,1)}) %all-gather.3.cloned.1.call-update) | async-done | bytes 1048592 | tf_op jit(solution)/shard_map/all_gather | solution.py:125
  360.6 9.0 %convolution_convert_fusion.1 = bf16[512,2048]{1,0:T(8,128)(2,1)} fusion(bf16[512,1024]{0,1:T(8,128)(2,1)} %all-gather.3.cloned.1.call-done, f32[256,8,8,128]{3,2,1,0:T(8,128)} %bitcast.171, bf16[2048,1024]{1,0:T(8,128)(2,1)} %param.8), kind=kOutput, calls=%fused_computation.65 | convolution fusion | flops 2154823680 | bytes 15728640 | tf_op jit(solution)/shard_map/dot_general | solution.py:124
  377.8 42.7 %all-to-all-done = bf16[4,128,2048]{2,1,0:T(8,128)(2,1)S(1)} async-done(((bf16[4,128,2048]{2,1,0:T(8,128)(2,1)}), bf16[4,128,2048]{2,1,0:T(8,128)(2,1)S(1)}, u32[]{:S(2)}, u32[]{:S(2)}) %all-to-all-start) | async-done | bytes 2097184 | tf_op jit(solution)/shard_map/all_to_all | solution.py:130
  421.9 66.5 %all-reduce.2.cloned.1.call-done = f32[2048,1024]{1,0:T(8,128)} async-done(((f32[2048,1024]{1,0:T(8,128)}), f32[2048,1024]{1,0:T(8,128)}) %all-reduce.2.cloned.1.call-update) | async-done | bytes 8388624 | tf_op jit(solution)/shard_map/psum | solution.py:138
  488.5 8.4 %copy.95 = f32[2048,1024]{1,0:T(8,128)} copy(f32[2048,1024]{1,0:T(8,128)} %all-reduce.2.cloned.1.call-done) | data formatting | bytes 16777216
  (125 shorter events, 92.9 us)
Async XLA Ops:
  7.2 113.1 %reduce-scatter.2.cloned.1.call-start = ((), (), s32[]{:S(2)}) async-start(), calls=%async_computation.2 | async-start | bytes 2621440 | tf_op jit(solution)/shard_map/reduce_scatter | solution.py:95
  12.8 18.1 %collective-permute-start.2 = (bf16[128,2048]{1,0:T(8,128)(2,1)S(1)}, bf16[128,2048]{1,0:T(8,128)(2,1)S(1)}, u32[]{:S(2)}, u32[]{:S(2)}) collective-permute-start(bf16[128,2048]{1,0:T(8,128)(2,1)S(1)} %bitcast.190), channel_id=1, source_target_pairs={{0,3},{1,2},{2,1},{3,0},{4,7},{5,6},{6,5},{7,4},{8,11},{9,10},{10,... | collective-permute-start | bytes 1572872 | tf_op jit(solution)/shard_map/ppermute | solution.py:91
  19.2 43.6 %collective-permute-start.1 = (bf16[128,2048]{1,0:T(8,128)(2,1)S(1)}, bf16[128,2048]{1,0:T(8,128)(2,1)}, u32[]{:S(2)}, u32[]{:S(2)}) collective-permute-start(bf16[128,2048]{1,0:T(8,128)(2,1)S(1)} %bitcast.191), channel_id=1, source_target_pairs={{0,2},{1,3},{2,0},{3,1},{4,6},{5,7},{6,4},{7,5},{8,10},{9,11},{10,... | collective-permute-start | bytes 1572872 | tf_op jit(solution)/shard_map/ppermute | solution.py:91
  19.5 43.3 %collective-permute-start = (bf16[128,2048]{1,0:T(8,128)(2,1)S(1)}, bf16[128,2048]{1,0:T(8,128)(2,1)}, u32[]{:S(2)}, u32[]{:S(2)}) collective-permute-start(bf16[128,2048]{1,0:T(8,128)(2,1)S(1)} %bitcast.192), channel_id=1, source_target_pairs={{0,1},{1,0},{2,3},{3,2},{4,5},{5,4},{6,7},{7,6},{8,9},{9,8},{10,11... | collective-permute-start | bytes 1572872 | tf_op jit(solution)/shard_map/ppermute | solution.py:91
  30.9 32.0 %copy-start.14 = (bf16[128,2048]{1,0:T(8,128)(2,1)}, bf16[128,2048]{1,0:T(8,128)(2,1)S(1)}, u32[]{:S(2)}) copy-start(bf16[128,2048]{1,0:T(8,128)(2,1)S(1)} %collective-permute-done.2) | copy-start | bytes 1572868
  66.5 4.9 copy-start.1
  66.5 5.9 %copy-start.2 = (bf16[4,128,2048]{2,1,0:T(8,128)(2,1)S(1)}, bf16[4,128,2048]{2,1,0:T(8,128)(2,1)}, u32[]{:S(2)}) copy-start(bf16[4,128,2048]{2,1,0:T(8,128)(2,1)} %gather_fusion) | copy-start | bytes 6291460
  67.1 4.3 copy-start
  76.4 51.9 %copy-start.6 = (bf16[128,4096]{1,0:T(8,128)(2,1)S(1)}, bf16[128,4096]{1,0:T(8,128)(2,1)}, u32[]{:S(2)}) copy-start(bf16[128,4096]{1,0:T(8,128)(2,1)} %param.10) | copy-start | bytes 3145732
  76.4 53.2 %copy-start.7 = (bf16[128,4096]{1,0:T(8,128)(2,1)S(1)}, bf16[128,4096]{1,0:T(8,128)(2,1)}, u32[]{:S(2)}) copy-start(bf16[128,4096]{1,0:T(8,128)(2,1)} %param.11) | copy-start | bytes 3145732
  76.4 254.4 %all-gather.5.cloned.1.call-start = ((), (), s32[]{:S(2)}) async-start(), calls=%async_computation.4 | async-start | bytes 1310720 | tf_op jit(solution)/shard_map/all_gather | solution.py:134
  121.4 8.9 %collective-permute-start.4 = (bf16[128,1024]{1,0:T(8,128)(2,1)S(1)}, bf16[128,1024]{1,0:T(8,128)(2,1)S(1)}, u32[]{:S(2)}, u32[]{:S(2)}) collective-permute-start(bf16[128,1024]{1,0:T(8,128)(2,1)S(1)} %convert_element_type.32), channel_id=1, source_target_pairs={{0,1},{1,2},{2,3},{3,4},{4,5},{5,6},{6,7},{7,8},{8,9},{9,10},{10,1... | collective-permute-start | bytes 786440 | tf_op jit(solution)/shard_map/ppermute | solution.py:28
  124.0 10.4 %collective-permute-start.3 = (bf16[128,1024]{1,0:T(8,128)(2,1)S(1)}, bf16[128,1024]{1,0:T(8,128)(2,1)}, u32[]{:S(2)}, u32[]{:S(2)}) collective-permute-start(bf16[128,1024]{1,0:T(8,128)(2,1)S(1)} %convert_element_type.32), channel_id=1, source_target_pairs={{0,2},{1,3},{2,4},{3,5},{4,6},{5,7},{6,8},{7,9},{8,10},{9,11},{10,... | collective-permute-start | bytes 786440 | tf_op jit(solution)/shard_map/ppermute | solution.py:28
  136.8 6.1 %copy-start.4 = (bf16[4,384,128]{2,1,0:T(8,128)(2,1)}, bf16[4,384,128]{2,1,0:T(8,128)(2,1)S(1)}, u32[]{:S(2)}) copy-start(bf16[4,384,128]{2,1,0:T(8,128)(2,1)S(1)} %get-tuple-element.264) | copy-start | bytes 1179652 | tf_op jit(solution)/shard_map/while
  164.7 6.1 %copy-start.4 = (bf16[4,384,128]{2,1,0:T(8,128)(2,1)}, bf16[4,384,128]{2,1,0:T(8,128)(2,1)S(1)}, u32[]{:S(2)}) copy-start(bf16[4,384,128]{2,1,0:T(8,128)(2,1)S(1)} %get-tuple-element.264) | copy-start | bytes 1179652 | tf_op jit(solution)/shard_map/while
  192.6 6.1 %copy-start.4 = (bf16[4,384,128]{2,1,0:T(8,128)(2,1)}, bf16[4,384,128]{2,1,0:T(8,128)(2,1)S(1)}, u32[]{:S(2)}) copy-start(bf16[4,384,128]{2,1,0:T(8,128)(2,1)S(1)} %get-tuple-element.264) | copy-start | bytes 1179652 | tf_op jit(solution)/shard_map/while
  220.5 6.1 %copy-start.4 = (bf16[4,384,128]{2,1,0:T(8,128)(2,1)}, bf16[4,384,128]{2,1,0:T(8,128)(2,1)S(1)}, u32[]{:S(2)}) copy-start(bf16[4,384,128]{2,1,0:T(8,128)(2,1)S(1)} %get-tuple-element.264) | copy-start | bytes 1179652 | tf_op jit(solution)/shard_map/while
  248.4 5.1 %copy-start.11 = (bf16[4,128,8,128]{3,1,2,0:T(8,128)(2,1)}, bf16[4,128,8,128]{3,1,2,0:T(8,128)(2,1)S(1)}, u32[]{:S(2)}) copy-start(bf16[4,128,8,128]{3,1,2,0:T(8,128)(2,1)S(1)} %get-tuple-element.59) | copy-start | bytes 3145732
  250.9 35.2 %collective-permute-start.6 = (f32[128,1024]{0,1:T(8,128)}, f32[128,1024]{0,1:T(8,128)}, u32[]{:S(2)}, u32[]{:S(2)}) collective-permute-start(f32[128,1024]{0,1:T(8,128)} %get-tuple-element.149), channel_id=1, source_target_pairs={{2,0},{3,1},{4,2},{5,3},{6,4},{7,5},{8,6},{9,7},{10,8},{11,9},{12,... | collective-permute-start | bytes 1572872 | tf_op jit(solution)/shard_map/ppermute | solution.py:28
  252.2 33.9 %collective-permute-start.5 = (f32[128,1024]{0,1:T(8,128)}, f32[128,1024]{0,1:T(8,128)}, u32[]{:S(2)}, u32[]{:S(2)}) collective-permute-start(f32[128,1024]{0,1:T(8,128)} %get-tuple-element.148), channel_id=1, source_target_pairs={{1,0},{2,1},{3,2},{4,3},{5,4},{6,5},{7,6},{8,7},{9,8},{10,9},{11,1... | collective-permute-start | bytes 1572872 | tf_op jit(solution)/shard_map/ppermute | solution.py:28
  253.5 77.3 %copy-start.3 = (bf16[4,128,2048]{2,1,0:T(8,128)(2,1)S(1)}, bf16[4,128,2048]{2,1,0:T(8,128)(2,1)}, u32[]{:S(2)}) copy-start(bf16[4,128,2048]{2,1,0:T(8,128)(2,1)} %gather_fusion) | copy-start | bytes 6291460
  288.4 72.3 %all-gather.3.cloned.1.call-start = ((), (), s32[]{:S(2)}) async-start(), calls=%async_computation.3 | async-start | bytes 1310720 | tf_op jit(solution)/shard_map/all_gather | solution.py:125
  289.1 199.4 %all-reduce.2.cloned.1.call-start = ((), (), s32[]{:S(2)}) async-start(), calls=%async_computation.5 | async-start | bytes 16777216 | tf_op jit(solution)/shard_map/psum | solution.py:138
  369.7 50.8 %all-to-all-start = ((bf16[4,128,2048]{2,1,0:T(8,128)(2,1)}), bf16[4,128,2048]{2,1,0:T(8,128)(2,1)S(1)}, u32[]{:S(2)}, u32[]{:S(2)}) async-start(bf16[4,128,2048]{2,1,0:T(8,128)(2,1)} %bitcast.22), calls=%async_computation.1 | async-start | bytes 4194304 | tf_op jit(solution)/shard_map/all_to_all | solution.py:130
  (16 other events, 45.4 us)
Sparse Core Ops, SparseCore 0:
  76.5 43.7 reduce-scatter.1
  288.5 42.2 all-gather.4
  332.4 28.2 all-gather.2
  364.0 124.4 all-reduce.1
